TPU v7x, 256 devices: a whole 4x4x8 slice. The times are simulated.
256 devices in a mesh: section: 2 (over core), rep: 8 (over z_lo, x), tp: 16 (over z_hi, y).
Axes of the slice: x: 4, y: 4, z: 8 (z_hi: 4, z_lo: 2; z = z_hi * 2 + z_lo), core: 2. Of those that a mesh axis runs over, the one named last changes fastest.
Arguments:
- states: bfloat16 [2, 8, 256, 8192], P('section', 'rep', None, 'tp'), may hold values from -6 to 6
- q_weight: bfloat16 [8192, 4096], P(None, 'tp'), may hold values from -0.0625 to 0.0625
- kv_weight: bfloat16 [8192, 1024], P('tp'), may hold values from -0.0625 to 0.0625
- o_weight: bfloat16 [4096, 8192], P(None, 'tp'), may hold values from -0.09375 to 0.09375
- store_keys: bfloat16 [2, 8, 4096, 512], P('section', 'rep', 'tp'), may hold values from -170 to 170
- store_values: bfloat16 [2, 8, 4096, 512], P('section', 'rep', 'tp'), may hold values from -48 to 48
- prefix_len: int32 [8], replicated, may hold values from 1024 to 4096
- cache_len: int32 [8, 4], P('rep'), may hold values from 128 to 1024
- parents: int32 [8, 4, 64], P('rep'), may hold values from -1 to 62, as said below
Outputs:
- attn_out: bfloat16 [2, 8, 256, 8192], P('section', 'rep', None, 'tp')
Inputs may be any that keep to these rules, and one draw needn't show every extreme that they name: `parents`: each node's parent is an earlier node of the same tree; only node 0 has -1.
All inputs are finite; a program needn't handle non-finite values.
Results may differ from a plain program's by a relative error of at most 0.0065.
The roundings to bfloat16 on the way count: a program that leaves them out, or rounds other values in their place, can miss the bound.
Values may be sent and summed in bfloat16 or wider, within the bound.
A program may use at most 64 MiB of HBM per device.

v0:
```python
import jax
import jax.numpy as jnp
from jax import lax
from jax.sharding import Mesh
from jax.sharding import PartitionSpec as P

HD = 128
SEQS = 4
NODES = 64
CACHE = 1024
TP = ("tp_0", "tp_1")


ROPE_BASE = 500000.0
MASKED_SCORE = -1e30


def in_blocks(shard, dim, devices):
    before, after = (shard.shape[:dim], shard.shape[dim + 1 :])
    return jnp.moveaxis(shard.reshape(*before, devices, -1, *after), dim, 0)


def summed_on_arrival(shard, axis, dim):
    tiles = in_blocks(shard, dim, lax.axis_size(axis))
    arrived = lax.all_to_all(tiles, axis, split_axis=0, concat_axis=0, tiled=True)
    return arrived.astype(jnp.float32).sum(axis=0)


def passed_along(block, axis, distance):
    devices = range(lax.axis_size(axis))
    route = [(i - distance, i) for i in devices if i - distance in devices]
    return lax.ppermute(block, axis, route)


def joined_along(tiles, dim):
    lengths = list(tiles.shape[1:])
    lengths[dim] *= tiles.shape[0]
    return jnp.moveaxis(tiles, 0, dim).reshape(lengths)


def exchange_in_order(tiles, axes, order):
    lengths = [lax.axis_size(a) for a in axes]
    tiles = tiles.reshape(*lengths, *tiles.shape[1:])
    for k in order:
        tiles = lax.all_to_all(tiles, axes[k], split_axis=k, concat_axis=k, tiled=True)
    return tiles.reshape(-1, *tiles.shape[len(axes) :])


def exchange_by_axis(shard, axes, order, split_dim, concat_dim):
    tiles = in_blocks(shard, split_dim, lax.axis_size(axes))
    return joined_along(exchange_in_order(tiles, axes, order), concat_dim)


def rotate(vectors, positions):
    head_size = vectors.shape[-1]
    half_width = head_size // 2
    exponent = jnp.arange(half_width, dtype=jnp.float32) * (-2.0 / head_size)
    frequency = jnp.exp(exponent * jnp.log(jnp.float32(ROPE_BASE)))
    angles = positions.astype(jnp.float32)[:, None] * frequency[None, :]
    cosine = jnp.cos(angles)[:, None, :]
    sine_of = jnp.sin(angles)[:, None, :]
    front_half = vectors[..., :half_width]
    back_half = vectors[..., half_width:]
    return jnp.concatenate(
        [front_half * cosine - back_half * sine_of, back_half * cosine + front_half * sine_of],
        axis=-1,
    )


def closure(parents):
    node_count = parents.shape[-1]
    node_ids = jnp.arange(node_count, dtype=jnp.int32)
    reached = (parents[:, :, None] == node_ids[None, None, :]).astype(jnp.float32)
    reached = reached + jnp.eye(node_count, dtype=jnp.float32)[None]
    for level_index in range(max(1, (node_count - 1).bit_length())):
        reached = jnp.minimum(
            jnp.einsum("sij,sjk->sik", reached, reached, precision=lax.Precision.HIGHEST), 1.0
        )
    return reached


def partial_attend(queries, all_keys, all_values, visible):
    row_count = queries.shape[0]
    kv_heads = all_keys.shape[1] // HD
    group_size = queries.shape[1] // all_keys.shape[1]
    row_tops = []
    row_totals = []
    mixtures = []
    for kv_head in range(kv_heads):
        query_block = queries[
            :, kv_head * group_size * HD : (kv_head + 1) * group_size * HD
        ].reshape(row_count * group_size, HD)
        key_block = all_keys[:, kv_head * HD : (kv_head + 1) * HD]
        value_block = all_values[:, kv_head * HD : (kv_head + 1) * HD]
        scores = lax.dot_general(
            query_block, key_block, (((1,), (1,)), ((), ())), preferred_element_type=jnp.float32
        )
        scores = scores.reshape(row_count, group_size, -1) * HD ** (-0.5)
        scores = jnp.where(visible[:, None, :], scores, MASKED_SCORE)
        row_top = jnp.max(scores, axis=-1)
        weights = jnp.where(visible[:, None, :], jnp.exp(scores - row_top[..., None]), 0.0)
        row_total = jnp.sum(weights, axis=-1)
        mixed_rows = jnp.dot(
            weights.astype(jnp.bfloat16).reshape(row_count * group_size, -1),
            value_block,
            preferred_element_type=jnp.float32,
        )
        mixed_rows = (
            mixed_rows.reshape(row_count, group_size, HD) / jnp.maximum(row_total, 1.0)[..., None]
        )
        row_tops.append(row_top)
        row_totals.append(row_total)
        mixtures.append(mixed_rows.reshape(row_count, group_size * HD).astype(jnp.bfloat16))
    return (
        jnp.concatenate(row_tops, axis=1),
        jnp.concatenate(row_totals, axis=1),
        jnp.concatenate(mixtures, axis=1),
    )


def finish(tops, totals, parts):
    piece_count, row_count, head_count = tops.shape
    best = jnp.max(tops, axis=0)
    factor = jnp.exp(tops - best[None]) * totals
    denominator = jnp.sum(factor, axis=0)
    numerator = jnp.sum(
        parts.astype(jnp.float32).reshape(piece_count, row_count, head_count, HD)
        * factor[..., None],
        axis=0,
    )
    return (
        (numerator / denominator[..., None])
        .reshape(row_count, head_count * HD)
        .astype(jnp.bfloat16)
    )


def per_device(
    states, q_weight, kv_weight, o_weight, store_keys, store_values, prefix_len, cache_len, parents
):
    inputs = states[0, 0]
    row_count = inputs.shape[0]
    tp_count = lax.axis_size(TP)
    tp_index = lax.axis_index(TP)
    replica = lax.axis_index("rep")
    rep_count = lax.axis_size("rep")
    decoding = lax.axis_index("section") == 1
    own_cols = q_weight.shape[1]
    kv_width = kv_weight.shape[1] // 2
    block_rows = row_count // tp_count
    first_row = tp_index * block_rows
    row_ids = jnp.arange(row_count, dtype=jnp.int32)
    seq_of = row_ids // NODES
    own_prefix = prefix_len[replica]
    reached = closure(parents[0])
    depths = (jnp.sum(reached, axis=-1).astype(jnp.int32) - 1).reshape(row_count)
    seq_lengths = jnp.broadcast_to(cache_len[0][:, None], (SEQS, NODES)).reshape(row_count)
    tree_base = jnp.where(seq_of == 0, own_prefix + row_count, seq_lengths)
    positions = jnp.where(decoding, tree_base + depths, own_prefix + row_ids)
    weight_rows = q_weight
    query_sums = jnp.dot(
        lax.all_gather(inputs, TP, axis=1, tiled=True),
        weight_rows,
        preferred_element_type=jnp.float32,
    )
    own_queries = (
        rotate(query_sums.reshape(row_count, own_cols // HD, HD), positions)
        .reshape(row_count, own_cols)
        .astype(jnp.bfloat16)
    )
    queries = lax.all_gather(own_queries, TP, axis=1, tiled=True)
    kv_rows = summed_on_arrival(
        jnp.dot(inputs, kv_weight, preferred_element_type=jnp.float32).astype(jnp.bfloat16), TP, 0
    )
    local_pos = lax.dynamic_slice_in_dim(positions, first_row, block_rows, 0)
    new_keys = (
        rotate(kv_rows[:, :kv_width].reshape(block_rows, -1, HD), local_pos)
        .reshape(block_rows, kv_width)
        .astype(jnp.bfloat16)
    )
    new_values = kv_rows[:, kv_width:].astype(jnp.bfloat16)
    moved = passed_along(jnp.stack([new_keys, new_values]), ("section", "rep"), rep_count)
    tail_keys = moved[0]
    tail_values = moved[1]
    store_rows = store_keys.shape[2]
    store_pos = tp_index * store_rows + jnp.arange(store_rows, dtype=jnp.int32)
    prefill_store = jnp.broadcast_to(store_pos[None, :] < own_prefix, (row_count, store_rows))
    decode_store = (store_pos[None, :] // CACHE == seq_of[:, None]) & (
        store_pos[None, :] % CACHE < seq_lengths[:, None]
    )
    block_ids = first_row + jnp.arange(block_rows, dtype=jnp.int32)
    prefill_new = block_ids[None, :] <= row_ids[:, None]
    eye_seq = (jnp.arange(SEQS)[:, None] == jnp.arange(SEQS)[None, :]).astype(jnp.float32)
    tree_full = (eye_seq[:, None, :, None] * reached[:, :, None, :]).reshape(row_count, row_count)
    decode_new = lax.dynamic_slice_in_dim(tree_full, first_row, block_rows, 1) > 0.5
    tail_seen = jnp.broadcast_to((seq_of == 0)[:, None], (row_count, block_rows))
    decode_mask = jnp.concatenate([decode_store, decode_new, tail_seen], axis=1)
    prefill_mask = jnp.concatenate([prefill_store, prefill_new, jnp.zeros_like(tail_seen)], axis=1)
    visible = jnp.where(decoding, decode_mask, prefill_mask)
    all_keys = jnp.concatenate([store_keys[0, 0], new_keys, tail_keys], axis=0)
    all_values = jnp.concatenate([store_values[0, 0], new_values, tail_values], axis=0)
    row_tops, row_totals, mixtures = partial_attend(queries, all_keys, all_values, visible)
    peer_tops, peer_totals, peer_mix = (
        exchange_by_axis(row_tops[None], TP, (0, 1), 2, 0),
        exchange_by_axis(row_totals[None], TP, (0, 1), 2, 0),
        exchange_by_axis(mixtures[None].astype(jnp.float32), TP, (0, 1), 2, 0).astype(jnp.bfloat16),
    )
    own_attended = finish(peer_tops, peer_totals, peer_mix)
    weight_rows = o_weight
    result = jnp.dot(
        lax.all_gather(own_attended, TP, axis=1, tiled=True),
        weight_rows,
        preferred_element_type=jnp.float32,
    )
    return result.astype(jnp.bfloat16)[None, None]


def solution(mesh):
    split = Mesh(
        mesh.devices.reshape(mesh.shape["section"], mesh.shape["rep"], 4, 4),
        ("section", "rep", "tp_0", "tp_1"),
    )
    placed = (
        P("section", "rep", None, TP),
        P(None, TP),
        P(TP, None),
        P(None, TP),
        P("section", "rep", TP, None),
        P("section", "rep", TP, None),
        P(),
        P("rep", None),
        P("rep", None, None),
    )
    return jax.shard_map(
        per_device,
        mesh=split,
        in_specs=placed,
        out_specs=P("section", "rep", None, TP),
        check_vma=False,
    )
```

profile of v0, /device:TPU:2, one launch (start us, length us, event | category | flops | bytes accessed | tf_op | source)
XLA Modules:
  0.0 364.5 jit_solution(4483975345601718534)
XLA Ops:
  13.1 81.5 %all-gather.9.cloned.1.call-done = bf16[1,1,256,8192]{3,2,1,0:T(8,128)(2,1)} async-done(((bf16[1,1,256,512]{3,2,1,0:T(8,128)(2,1)}), bf16[1,1,256,8192]{3,2,1,0:T(8,128)(2,1)}) %all-gather.9.cloned.1.call-update) | async-done | bytes 4194320 | tf_op jit(solution)/shard_map/all_gather | solution.py:162
  94.6 5.2 %fusion = f32[256,256]{0,1:T(8,128)S(1)} fusion(bf16[8192,256]{1,0:T(8,128)(2,1)} %param.10, bf16[1,1,256,8192]{3,2,1,0:T(8,128)(2,1)} %all-gather.9.cloned.1.call-done), kind=kOutput, calls=%fused_computation | convolution fusion | flops 1073741824 | bytes 8650752 | tf_op jit(solution)/shard_map/dot_general | solution.py:161
  101.8 6.2 %all-to-all-start = ((bf16[16,16,1024]{2,1,0:T(8,128)(2,1)}), bf16[16,16,1024]{2,1,0:T(8,128)(2,1)S(1)}, u32[]{:S(2)}, u32[]{:S(2)}) async-start(bf16[16,16,1024]{2,1,0:T(8,128)(2,1)} %bitcast.9), calls=%async_computation | async-start | bytes 1048576 | tf_op jit(solution)/shard_map/all_to_all | solution.py:25
  110.0 18.6 %all-to-all-done = bf16[16,16,1024]{2,1,0:T(8,128)(2,1)S(1)} async-done(((bf16[16,16,1024]{2,1,0:T(8,128)(2,1)}), bf16[16,16,1024]{2,1,0:T(8,128)(2,1)S(1)}, u32[]{:S(2)}, u32[]{:S(2)}) %all-to-all-start) | async-done | bytes 524320 | tf_op jit(solution)/shard_map/all_to_all | solution.py:25
  131.9 31.4 %all-gather.5.cloned.1.call-done = bf16[256,4096]{0,1:T(8,128)(2,1)} async-done(((bf16[256,256]{0,1:T(8,128)(2,1)}), bf16[256,4096]{0,1:T(8,128)(2,1)}) %all-gather.5.cloned.1.call-update) | async-done | bytes 2097168 | tf_op jit(solution)/shard_map/all_gather | solution.py:171
  163.3 1.7 fusion.71
  166.5 3.3 fusion.6
  171.0 4.7 %all-to-all-start.3 = ((f32[4,4,1,256,2]{3,4,1,2,0:T(2,128)}), f32[4,4,1,256,2]{3,4,1,2,0:T(2,128)S(1)}, u32[]{:S(2)}, u32[]{:S(2)}) async-start(f32[4,4,1,256,2]{3,4,1,2,0:T(2,128)} %bitcast.32), calls=%async_computation.3 | async-start | bytes 65536 | tf_op jit(solution)/shard_map/all_to_all | solution.py:45
  175.7 4.3 %fusion.8 = (f32[256,8]{0,1:T(8,128)S(1)}, f32[256,8]{0,1:T(8,128)S(1)}, f32[256,8]{0,1:T(8,128)S(1)}) fusion(f32[256,8,288]{0,2,1:T(8,128)} %get-tuple-element.32, f32[256,8]{0,1:T(8,128)S(1)} %get-tuple-element.6, pred[256,288]{0,1:T(8,128)(4,1)S(1)} %add_select_fusion, f32[256,8]{0,1:T(8,128)S(1)} %get-tuple-element.7, f32[256,8,288]{0,2,1:T(8,128)} %copy-done.1, ...), kind=kLoop, calls=%fused_computation.19 | loop fusion | flops 8841216 | bytes 7200768 | tf_op jit(solution)/shard_map/reduce_sum | solution.py:102
  181.7 1.6 fusion.15
  186.2 7.2 %all-to-all-start.5 = ((f32[4,4,1,256,2]{3,4,1,2,0:T(2,128)}), f32[4,4,1,256,2]{3,4,1,2,0:T(2,128)S(1)}, u32[]{:S(2)}, u32[]{:S(2)}) async-start(f32[4,4,1,256,2]{3,4,1,2,0:T(2,128)} %bitcast.123), calls=%async_computation.5 | async-start | bytes 65536 | tf_op jit(solution)/shard_map/all_to_all | solution.py:45
  193.3 2.5 fusion.17
  196.4 4.8 %all-to-all-done.5 = f32[4,4,1,256,2]{3,4,1,2,0:T(2,128)S(1)} async-done(((f32[4,4,1,256,2]{3,4,1,2,0:T(2,128)}), f32[4,4,1,256,2]{3,4,1,2,0:T(2,128)S(1)}, u32[]{:S(2)}, u32[]{:S(2)}) %all-to-all-start.5) | async-done | bytes 32800 | tf_op jit(solution)/shard_map/all_to_all | solution.py:45
  201.2 3.4 all-to-all-start.4
  204.6 3.1 maximum_convert_fusion
  207.7 2.3 all-to-all-done.4
  210.0 3.6 all-to-all-start.1
  214.3 45.5 %all-to-all-done.1 = bf16[4,4,1,256,256]{3,4,1,2,0:T(8,128)(2,1)S(1)} async-done(((bf16[4,4,1,256,256]{3,4,1,2,0:T(8,128)(2,1)}), bf16[4,4,1,256,256]{3,4,1,2,0:T(8,128)(2,1)S(1)}, u32[]{:S(2)}, u32[]{:S(2)}) %all-to-all-start.1) | async-done | bytes 2097184 | tf_op jit(solution)/shard_map/all_to_all | solution.py:45
  259.8 3.4 all-to-all-start.6
  264.6 4.0 %all-to-all-done.6 = f32[4,4,1,256,2]{3,4,0,2,1:T(2,128)S(1)} async-done(((f32[4,4,1,256,2]{3,4,0,2,1:T(2,128)}), f32[4,4,1,256,2]{3,4,0,2,1:T(2,128)S(1)}, u32[]{:S(2)}, u32[]{:S(2)}) %all-to-all-start.6) | async-done | bytes 32800 | tf_op jit(solution)/shard_map/all_to_all | solution.py:45
  268.6 3.6 all-to-all-start.2
  272.4 22.8 %all-to-all-done.2 = bf16[4,4,1,256,256]{3,4,0,2,1:T(8,128)(2,1)S(1)} async-done(((bf16[4,4,1,256,256]{3,4,0,2,1:T(8,128)(2,1)}), bf16[4,4,1,256,256]{3,4,0,2,1:T(8,128)(2,1)S(1)}, u32[]{:S(2)}, u32[]{:S(2)}) %all-to-all-start.2) | async-done | bytes 2097184 | tf_op jit(solution)/shard_map/all_to_all | solution.py:45
  296.7 56.5 %all-gather.7.cloned.1.call-done = bf16[256,4096]{0,1:T(8,128)(2,1)} async-done(((bf16[256,256]{0,1:T(8,128)(2,1)}), bf16[256,4096]{0,1:T(8,128)(2,1)}) %all-gather.7.cloned.1.call-update) | async-done | bytes 2097168 | tf_op jit(solution)/shard_map/all_gather | solution.py:211
  353.2 4.8 %fusion.42 = bf16[1,1,256,512]{3,2,1,0:T(8,128)(2,1)} fusion(bf16[256,4096]{0,1:T(8,128)(2,1)} %all-gather.7.cloned.1.call-done, bf16[4096,512]{1,0:T(8,128)(2,1)} %param.12), kind=kOutput, calls=%fused_computation.55 | convolution fusion | flops 1073872896 | bytes 6553600 | tf_op jit(solution)/shard_map/dot_general | solution.py:210
  (109 shorter events, 24.4 us)
Async XLA Ops:
  6.5 94.0 %copy-start = (bf16[512,1024]{1,0:T(8,128)(2,1)S(1)}, bf16[512,1024]{1,0:T(8,128)(2,1)}, u32[]{:S(2)}) copy-start(bf16[512,1024]{1,0:T(8,128)(2,1)} %param.11) | copy-start | bytes 3145732
  6.5 4.2 %copy-start.13 = (s32[8]{0:T(128)S(1)}, s32[8]{0:T(128)}, u32[]{:S(2)}) copy-start(s32[8]{0:T(128)} %param.15) | copy-start | bytes 100
  6.5 88.1 %all-gather.9.cloned.1.call-start = ((), (), s32[]{:S(2)}) async-start(), calls=%async_computation.9 | async-start | bytes 4456448 | tf_op jit(solution)/shard_map/all_gather | solution.py:162
  7.3 156.1 %all-gather.5.cloned.1.call-start = ((), (), s32[]{:S(2)}) async-start(), calls=%async_computation.7 | async-start | bytes 2228224 | tf_op jit(solution)/shard_map/all_gather | solution.py:171
  13.1 87.5 %copy-start.6 = (bf16[1,1,256,512]{3,2,1,0:T(8,128)(2,1)S(1)}, bf16[1,1,256,512]{3,2,1,0:T(8,128)(2,1)}, u32[]{:S(2)}) copy-start(bf16[1,1,256,512]{3,2,1,0:T(8,128)(2,1)} %param.9) | copy-start | bytes 786436
  101.8 29.2 %copy-start.9 = (bf16[1,1,256,512]{3,2,1,0:T(8,128)(2,1)S(1)}, bf16[1,1,256,512]{3,2,1,0:T(8,128)(2,1)}, u32[]{:S(2)}) copy-start(bf16[1,1,256,512]{3,2,1,0:T(8,128)(2,1)} %param.13) | copy-start | bytes 786436
  101.8 29.2 %copy-start.10 = (bf16[1,1,256,512]{3,2,1,0:T(8,128)(2,1)S(1)}, bf16[1,1,256,512]{3,2,1,0:T(8,128)(2,1)}, u32[]{:S(2)}) copy-start(bf16[1,1,256,512]{3,2,1,0:T(8,128)(2,1)} %param.14) | copy-start | bytes 786436
  101.8 26.7 %all-to-all-start = ((bf16[16,16,1024]{2,1,0:T(8,128)(2,1)}), bf16[16,16,1024]{2,1,0:T(8,128)(2,1)S(1)}, u32[]{:S(2)}, u32[]{:S(2)}) async-start(bf16[16,16,1024]{2,1,0:T(8,128)(2,1)} %bitcast.9), calls=%async_computation | async-start | bytes 1048576 | tf_op jit(solution)/shard_map/all_to_all | solution.py:25
  128.9 2.1 collective-permute-start
  163.3 1.7 copy-start.7
  166.0 3.8 %copy-start.1 = (f32[256,8,288]{0,2,1:T(8,128)}, f32[256,8,288]{0,2,1:T(8,128)S(1)}, u32[]{:S(2)}) copy-start(f32[256,8,288]{0,2,1:T(8,128)S(1)} %fusion.48) | copy-start | bytes 7077892
  166.5 3.3 copy-start.3
  169.8 10.2 %copy-start.11 = (f32[256,8]{0,1:T(8,128)}, f32[256,8]{0,1:T(8,128)S(1)}, u32[]{:S(2)}) copy-start(f32[256,8]{0,1:T(8,128)S(1)} %get-tuple-element.8) | copy-start | bytes 24580
  171.0 15.2 %all-to-all-start.3 = ((f32[4,4,1,256,2]{3,4,1,2,0:T(2,128)}), f32[4,4,1,256,2]{3,4,1,2,0:T(2,128)S(1)}, u32[]{:S(2)}, u32[]{:S(2)}) async-start(f32[4,4,1,256,2]{3,4,1,2,0:T(2,128)} %bitcast.32), calls=%async_computation.3 | async-start | bytes 65536 | tf_op jit(solution)/shard_map/all_to_all | solution.py:45
  175.6 4.3 %copy-start.4 = (f32[256,8,288]{0,2,1:T(8,128)S(1)}, f32[256,8,288]{0,2,1:T(8,128)}, u32[]{:S(2)}) copy-start(f32[256,8,288]{0,2,1:T(8,128)} %copy-done.3) | copy-start | bytes 7077892
  175.7 4.3 %copy-start.8 = (bf16[288,512]{1,0:T(8,128)(2,1)S(1)}, bf16[288,512]{1,0:T(8,128)(2,1)}, u32[]{:S(2)}) copy-start(bf16[288,512]{1,0:T(8,128)(2,1)} %get-tuple-element.38) | copy-start | bytes 884740
  175.7 4.3 %copy-start.12 = (f32[256,8]{0,1:T(8,128)S(1)}, f32[256,8]{0,1:T(8,128)}, u32[]{:S(2)}) copy-start(f32[256,8]{0,1:T(8,128)} %broadcast_maximum_fusion.3) | copy-start | bytes 24580
  180.0 1.7 copy-start.5
  186.2 15.1 %all-to-all-start.5 = ((f32[4,4,1,256,2]{3,4,1,2,0:T(2,128)}), f32[4,4,1,256,2]{3,4,1,2,0:T(2,128)S(1)}, u32[]{:S(2)}, u32[]{:S(2)}) async-start(f32[4,4,1,256,2]{3,4,1,2,0:T(2,128)} %bitcast.123), calls=%async_computation.5 | async-start | bytes 65536 | tf_op jit(solution)/shard_map/all_to_all | solution.py:45
  201.2 8.8 %all-to-all-start.4 = ((f32[4,4,1,256,2]{3,4,0,2,1:T(2,128)}), f32[4,4,1,256,2]{3,4,0,2,1:T(2,128)S(1)}, u32[]{:S(2)}, u32[]{:S(2)}) async-start(f32[4,4,1,256,2]{3,4,0,2,1:T(2,128)} %copy.40), calls=%async_computation.4 | async-start | bytes 65536 | tf_op jit(solution)/shard_map/all_to_all | solution.py:45
  210.0 49.7 %all-to-all-start.1 = ((bf16[4,4,1,256,256]{3,4,1,2,0:T(8,128)(2,1)}), bf16[4,4,1,256,256]{3,4,1,2,0:T(8,128)(2,1)S(1)}, u32[]{:S(2)}, u32[]{:S(2)}) async-start(bf16[4,4,1,256,256]{3,4,1,2,0:T(8,128)(2,1)} %bitcast.109), calls=%async_computation.1 | async-start | bytes 4194304 | tf_op jit(solution)/shard_map/all_to_all | solution.py:45
  259.8 8.8 %all-to-all-start.6 = ((f32[4,4,1,256,2]{3,4,0,2,1:T(2,128)}), f32[4,4,1,256,2]{3,4,0,2,1:T(2,128)S(1)}, u32[]{:S(2)}, u32[]{:S(2)}) async-start(f32[4,4,1,256,2]{3,4,0,2,1:T(2,128)} %copy.42), calls=%async_computation.6 | async-start | bytes 65536 | tf_op jit(solution)/shard_map/all_to_all | solution.py:45
  268.6 26.6 %all-to-all-start.2 = ((bf16[4,4,1,256,256]{3,4,0,2,1:T(8,128)(2,1)}), bf16[4,4,1,256,256]{3,4,0,2,1:T(8,128)(2,1)S(1)}, u32[]{:S(2)}, u32[]{:S(2)}) async-start(bf16[4,4,1,256,256]{3,4,0,2,1:T(8,128)(2,1)} %copy.38), calls=%async_computation.2 | async-start | bytes 4194304 | tf_op jit(solution)/shard_map/all_to_all | solution.py:45
  272.2 81.0 %all-gather.7.cloned.1.call-start = ((), (), s32[]{:S(2)}) async-start(), calls=%async_computation.8 | async-start | bytes 2228224 | tf_op jit(solution)/shard_map/all_gather | solution.py:211
  (1 other events, 1.7 us)
Sparse Core Ops, SparseCore 0:
  9.7 84.8 all-gather.8
  100.7 62.5 all-gather.4
  296.9 56.3 all-gather.6
where the time goes:
time: 365 us
  waiting for transfers between devices  269 us (74%)
  starting transfers between devices  33.4 us (9%)
  matrix products  25.7 us (7%)
  between operations  14.2 us (4%)
  other arithmetic  14.1 us (4%)
  local copies, waits for them, and re-layouts  8.3 us (2%)
    all_gather x1, waiting for transfers between devices, per_device(): lax.all_gather(inputs, TP, axis=1, tiled=True)  81.5 us
    all_to_all x6, waiting for transfers between devices, exchange_in_order(): lax.all_to_all(tiles, axes[k], split_axis=k, concat_axis=k, tiled=True)  79.4 us
    all_gather x1, waiting for transfers between devices, per_device(): lax.all_gather(own_attended, TP, axis=1, tiled=True)  56.5 us
    all_gather x1, waiting for transfers between devices, per_device(): queries = lax.all_gather(own_queries, TP, axis=1, tiled=True)  31.4 us
    all_to_all x6, starting transfers between devices, exchange_in_order(): lax.all_to_all(tiles, axes[k], split_axis=k, concat_axis=k, tiled=True)  25.8 us
    all_to_all x1, waiting for transfers between devices, summed_on_arrival(): lax.all_to_all(tiles, axis, split_axis=0, concat_axis=0, tiled=True)  18.6 us
  transfers between devices with their start and end apart: 11, of which 10 were waited for; matrix products, arithmetic and copies ran while one was open for 8% of the time, Pallas kernels for 0%

commit v1 on v0

v1 whole, which is shorter than its diff:
```python
import functools

import jax
import jax.numpy as jnp
import numpy as np
from jax import lax
from jax.experimental import pallas as pl
from jax.experimental.pallas import tpu as pltpu
from jax.sharding import PartitionSpec as P

MESH = pl.DeviceIdType.MESH
HD = 128
ROWS = 256
NODES = 64
ROPE_BASE = 500000.0
MASKED_SCORE = -1e30
F32 = jnp.float32
BF16 = jnp.bfloat16


def slot_of(dz, dy):
    return dy * 4 + dz


class Exchange:
    def __init__(self, view, send_sems, recv_sems, at, pending):
        self.view, self.send_sems, self.recv_sems = view, send_sems, recv_sems
        self.at, self.pending, self.used = at, pending, 0

    def send(self, src, dst_slot, half, dz, dy):
        copy = pltpu.make_async_remote_copy(
            src_ref=src,
            dst_ref=self.view(dst_slot, half),
            send_sem=self.send_sems.at[self.used],
            recv_sem=self.recv_sems.at[dst_slot, half],
            device_id={"tp": self.at(dz, dy)},
            device_id_type=MESH,
        )
        self.used += 1
        copy.start()
        self.pending.append(copy)

    def arrived(self, dz, dy, half):
        slot = slot_of(dz, dy)
        view = self.view(slot, half)
        pltpu.make_async_remote_copy(
            src_ref=view,
            dst_ref=view,
            send_sem=self.send_sems.at[0],
            recv_sem=self.recv_sems.at[slot, half],
            device_id={"tp": self.at(1, 0)},
            device_id_type=MESH,
        ).wait_recv()

    def own_z(self, half):
        self.send(self.view(0, half), slot_of(1, 0), half, 1, 0)
        self.send(self.view(0, half), slot_of(3, 0), half, -1, 0)

    def relay_z(self, half):
        src = self.view(slot_of(1 if half == 0 else 3, 0), half)
        self.send(src, slot_of(2, 0), half, 1 if half == 0 else -1, 0)

    def along_y(self, dz, half):
        src = self.view(slot_of(dz, 0), half)
        self.send(src, slot_of(dz, 1), half, 0, 1)
        self.send(src, slot_of(dz, 3), half, 0, -1)

    def relay_y(self, dz, half):
        src = self.view(slot_of(dz, 1 if half == 0 else 3), half)
        self.send(src, slot_of(dz, 2), half, 0, 1 if half == 0 else -1)

    def near_y(self, dz):
        self.arrived(dz, 1, 0)
        self.relay_y(dz, 0)
        self.arrived(dz, 3, 1)
        self.relay_y(dz, 1)
        self.arrived(dz, 3, 0)
        self.arrived(dz, 1, 1)

    def far_y(self, dz):
        self.arrived(dz, 2, 0)
        self.arrived(dz, 2, 1)


def dot(a, b, dims=((1,), (0,))):
    return lax.dot_general(a, b, (dims, ((), ())), preferred_element_type=F32)


def iota(shape, dim):
    return lax.broadcasted_iota(jnp.int32, shape, dim)


def kernel(
    prefix_ref, cache_ref, parents_ref, freq_ref, x_hbm, wq_hbm, wkv_hbm, wo_hbm, sk_hbm, sv_hbm,
    out_ref,
    xg, wq, wkv, wo, kvps, kvpr, kg, vg, relay, nkv, tail, qacc, qh, closed, cos_ref, sin_ref,
    top_ref, total_ref, mix_ref, ag, oacc,
    local, x_send, x_recv, k_send, k_recv, r_recv, p_send, p_recv, n_send, n_recv, t_sem, a_send, a_recv,
):
    tp = lax.axis_index("tp")
    sec = lax.axis_index("section")
    rep = lax.axis_index("rep")
    z, y = tp // 4, tp % 4

    def at(dz, dy):
        return ((z + dz + 4) % 4) * 4 + (y + dy + 4) % 4

    def head_cols(dz):
        return pl.ds(pl.multiple_of(((z + dz + 4) % 4) * HD, HD), HD)

    def load(src, dst, index):
        copy = pltpu.make_async_copy(src, dst, local.at[index])
        copy.start()
        return copy

    x_in = load(x_hbm, xg.at[0], 0)
    wkv_in = load(wkv_hbm, wkv, 1)
    wq_in = load(wq_hbm, wq, 2)
    k_in = load(sk_hbm.at[:, head_cols(0)], kg.at[0], 3)
    v_in = load(sv_hbm.at[:, head_cols(0)], vg.at[0], 4)
    wo_in = load(wo_hbm, wo, 5)

    barrier = pltpu.get_barrier_semaphore()
    peers = [(dz, dy) for dy in range(4) for dz in range(4) if (dz, dy) != (0, 0)]
    for dz, dy in peers:
        pl.semaphore_signal(barrier, inc=1, device_id={"tp": at(dz, dy)}, device_id_type=MESH)
    pl.semaphore_signal(barrier, inc=1, device_id={"section": 1 - sec}, device_id_type=MESH)
    pl.semaphore_wait(barrier, 16)

    pending = []
    xs = Exchange(lambda s, h: xg.at[s, h], x_send, x_recv, at, pending)
    ks = Exchange(lambda s, h: (kg if h == 0 else vg).at[s], k_send, k_recv, at, pending)
    ats = Exchange(lambda s, h: ag.at[s, h], a_send, a_recv, at, pending)

    x_in.wait()
    for half in range(2):
        xs.own_z(half)
        xs.along_y(0, half)

    wkv_in.wait()
    own_x = xg[0].reshape(ROWS, -1)
    for head in range(4):
        for kind in range(2):
            cols = pl.ds(kind * 512 + head * HD, HD)
            part = dot(own_x, wkv[:, cols]).astype(BF16)
            kvps[:, head, :, pl.ds(kind * HD, HD)] = part.reshape(4, NODES, HD)

    for dz in (1, -1):
        ks.send(sk_hbm.at[:, head_cols(dz)], slot_of(dz % 4, 0), 0, dz, 0)
        ks.send(sv_hbm.at[:, head_cols(dz)], slot_of(dz % 4, 0), 1, dz, 0)

    def to_relay(src, half, dz):
        copy = pltpu.make_async_remote_copy(
            src_ref=src,
            dst_ref=relay.at[half],
            send_sem=k_send.at[ks.used],
            recv_sem=r_recv.at[half],
            device_id={"tp": at(dz, 0)},
            device_id_type=MESH,
        )
        ks.used += 1
        copy.start()
        pending.append(copy)
        return copy

    relays = [to_relay(sk_hbm.at[:, head_cols(2)], 0, 1), to_relay(sv_hbm.at[:, head_cols(2)], 1, -1)]

    parts_in = []
    for n, (dz, dy) in enumerate(peers):
        copy = pltpu.make_async_remote_copy(
            src_ref=kvps.at[(y + dy) % 4, (z + dz) % 4],
            dst_ref=kvpr.at[slot_of(dz, dy)],
            send_sem=p_send.at[n],
            recv_sem=p_recv.at[slot_of(dz, dy)],
            device_id={"tp": at(dz, dy)},
            device_id_type=MESH,
        )
        copy.start()
        pending.append(copy)
        parts_in.append(copy)

    row = iota((ROWS, ROWS), 0)
    col = iota((ROWS, ROWS), 1)
    spread = (iota((NODES, ROWS), 1) % NODES == iota((NODES, ROWS), 0)).astype(BF16)
    parents = dot(parents_ref[...].astype(F32).astype(BF16), spread)
    own_seq = iota((4, ROWS), 1) // NODES == iota((4, ROWS), 0)
    parent = jnp.sum(jnp.where(own_seq, parents, 0.0), axis=0, keepdims=True)
    node = iota((1, ROWS), 1)
    parent_at = jnp.where(parent < 0.0, -1.0, parent + (node // NODES * NODES).astype(F32))
    child = (row.astype(F32) == parent_at).astype(BF16)
    eye = (row == col).astype(BF16)
    closed[...] = (dot(child, eye, ((0,), (0,))) + eye.astype(F32)).astype(BF16)

    def square(level, carry):
        closed[...] = jnp.minimum(dot(closed[...], closed[...]), 1.0).astype(BF16)
        return carry

    lax.fori_loop(0, 6, square, 0)
    depths = dot(closed[...], jnp.ones((ROWS, HD), BF16)).astype(jnp.int32) - 1
    wide_row = iota((ROWS, HD), 0)
    seq = wide_row // NODES
    prefix = prefix_ref[rep]
    base = jnp.full((ROWS, HD), prefix + ROWS, jnp.int32)
    for s in range(1, 4):
        base = jnp.where(seq == s, cache_ref[0, s], base)
    positions = sec * (base + depths) + (1 - sec) * (prefix + wide_row)
    angles = positions.astype(F32) * freq_ref[...]
    cos_ref[...] = jnp.cos(angles)
    lane = iota((ROWS, HD), 1)
    sin_ref[...] = jnp.where(lane < HD // 2, -jnp.sin(angles), jnp.sin(angles))

    def rotate(v, cosine, sine):
        return v * cosine + pltpu.roll(v, HD // 2, 1) * sine

    wq_in.wait()

    def project(dz, dy, first=False):
        source = pl.multiple_of(at(-dz, -dy) * 512, 512)
        part = dot(xg[slot_of(dz, dy)].reshape(ROWS, -1), wq[pl.ds(source, 512), :])
        qacc[...] = part if first else qacc[...] + part

    xs.near_y(0)
    project(0, 0, True)
    xs.arrived(1, 0, 0)
    xs.relay_z(0)
    xs.along_y(1, 0)
    xs.arrived(3, 0, 0)
    xs.along_y(3, 0)
    xs.arrived(3, 0, 1)
    xs.relay_z(1)
    xs.along_y(3, 1)
    xs.arrived(1, 0, 1)
    xs.along_y(1, 1)
    project(0, 1)
    project(0, 3)
    project(1, 0)
    project(3, 0)
    xs.far_y(0)
    project(0, 2)
    for half in range(2):
        relays[half].wait_recv()
        ks.send(relay.at[half], slot_of(2, 0), half, 1 if half == 0 else -1, 0)
    xs.near_y(1)
    xs.near_y(3)
    for half in range(2):
        xs.arrived(2, 0, half)
        xs.along_y(2, half)
    project(1, 1)
    project(1, 3)
    project(3, 1)
    project(3, 3)
    project(2, 0)

    k_in.wait()
    v_in.wait()
    for dz in (0, 1, 3):
        for half in range(2):
            if dz:
                ks.arrived(dz, 0, half)
            ks.along_y(dz, half)

    for copy in parts_in:
        copy.wait_recv()
    fresh = kvps[y, z].astype(F32)
    for dz, dy in peers:
        fresh = fresh + kvpr[slot_of(dz, dy)].astype(F32)
    rows = pl.ds(pl.multiple_of(y * NODES, NODES), NODES)
    fresh_keys = rotate(fresh[:, :HD], cos_ref[rows, :], sin_ref[rows, :])
    nkv[0, y] = fresh_keys.astype(BF16)
    nkv[1, y] = fresh[:, HD:].astype(BF16)

    xs.far_y(1)
    xs.far_y(3)
    project(1, 2)
    project(3, 2)

    news = []
    for dy in range(1, 4):
        copy = pltpu.make_async_remote_copy(
            src_ref=nkv.at[:, y],
            dst_ref=nkv.at[:, y],
            send_sem=n_send.at[dy],
            recv_sem=n_recv.at[dy],
            device_id={"tp": at(0, dy)},
            device_id_type=MESH,
        )
        copy.start()
        pending.append(copy)

    xs.near_y(2)
    project(2, 1)
    project(2, 3)
    for half in range(2):
        ks.arrived(2, 0, half)
        ks.along_y(2, half)
    for dy in range(1, 4):
        piece = nkv.at[:, (y + 4 - dy) % 4]
        pltpu.make_async_remote_copy(
            src_ref=piece,
            dst_ref=piece,
            send_sem=n_send.at[dy],
            recv_sem=n_recv.at[dy],
            device_id={"tp": at(0, dy)},
            device_id_type=MESH,
        ).wait_recv()
    swap = pltpu.make_async_remote_copy(
        src_ref=nkv,
        dst_ref=tail,
        send_sem=t_sem.at[0],
        recv_sem=t_sem.at[1],
        device_id={"section": 1 - sec},
        device_id_type=MESH,
    )
    swap.start()
    pending.append(swap)
    xs.far_y(2)
    project(2, 2)
    for head in range(2):
        qh[head] = rotate(qacc[:, head * HD : (head + 1) * HD], cos_ref[...], sin_ref[...]).astype(BF16)

    seq_wide = row // NODES

    def attend(pieces, first=False):
        def one_head(head, carry):
            queries = qh[head]
            scores = []
            for keys, _, visible in pieces:
                scores.append(jnp.where(visible(), dot(queries, keys(), ((1,), (1,))) * HD**-0.5, MASKED_SCORE))
            best = functools.reduce(jnp.maximum, scores)
            best = jnp.max(best, axis=1, keepdims=True)
            if not first:
                before = top_ref[head][:, :1]
                best = jnp.maximum(best, before)
                fade = jnp.exp(before - best)
            total = 0.0
            mix = 0.0
            for score, (_, values, _) in zip(scores, pieces):
                weights = jnp.exp(score - best)
                total = total + weights
                mix = mix + dot(weights.astype(BF16), values())
            total = jnp.sum(total, axis=1, keepdims=True)
            if not first:
                total = total + total_ref[head][:, :1] * fade
                mix = mix + mix_ref[head] * fade
            top_ref[head] = jnp.broadcast_to(best, (ROWS, HD))
            total_ref[head] = jnp.broadcast_to(total, (ROWS, HD))
            mix_ref[head] = mix
            return carry

        lax.fori_loop(0, 2, one_head, 0)

    def new_visible():
        reached = (closed[...].astype(F32) > 0.5).astype(jnp.int32)
        return sec * reached + (1 - sec) * (col <= row).astype(jnp.int32) > 0

    def tail_visible():
        return sec * (seq_wide == 0).astype(jnp.int32) > 0

    def stored(dz, dy):
        slot = slot_of(dz, dy)
        from_z, from_y = (z - dz + 4) % 4, (y - dy + 4) % 4

        def visible():
            in_prompt = prefix - (from_z * 4 + from_y) * ROWS
            in_cache = cache_ref[0, from_z] - from_y * ROWS
            mine = (seq_wide == from_z).astype(jnp.int32)
            return col < (1 - sec) * in_prompt + sec * in_cache * mine

        return (lambda: kg[slot], lambda: vg[slot], visible)

    attend([(lambda: nkv[0].reshape(ROWS, HD), lambda: nkv[1].reshape(ROWS, HD), new_visible)], True)
    for dz in (0, 1, 3, 2):
        ks.near_y(dz)
    attend([stored(dz, 0) for dz in range(4)])
    swap.wait_recv()
    attend([(lambda: tail[0].reshape(ROWS, HD), lambda: tail[1].reshape(ROWS, HD), tail_visible)])
    attend([stored(dz, 1) for dz in range(4)])
    attend([stored(dz, 3) for dz in range(4)])
    for dz in range(4):
        ks.far_y(dz)
    attend([stored(dz, 2) for dz in range(4)])
    for head in range(2):
        done = (mix_ref[head] / total_ref[head]).astype(BF16)
        ag[0, :, :, head * HD : (head + 1) * HD] = done.reshape(2, ROWS // 2, HD)

    for half in range(2):
        ats.own_z(half)
        ats.along_y(0, half)
    wo_in.wait()

    def finish(dz, dy, first=False):
        source = pl.multiple_of(at(-dz, -dy) * 256, 256)
        part = dot(ag[slot_of(dz, dy)].reshape(ROWS, -1), wo[pl.ds(source, 256), :])
        oacc[...] = part if first else oacc[...] + part

    finish(0, 0, True)
    ats.near_y(0)
    ats.arrived(1, 0, 0)
    ats.relay_z(0)
    ats.along_y(1, 0)
    ats.arrived(3, 0, 0)
    ats.along_y(3, 0)
    ats.arrived(3, 0, 1)
    ats.relay_z(1)
    ats.along_y(3, 1)
    ats.arrived(1, 0, 1)
    ats.along_y(1, 1)
    finish(0, 1)
    finish(0, 3)
    finish(1, 0)
    finish(3, 0)
    ats.far_y(0)
    finish(0, 2)
    for half in range(2):
        ats.arrived(2, 0, half)
        ats.along_y(2, half)
    ats.near_y(1)
    ats.near_y(3)
    finish(2, 0)
    finish(1, 1)
    finish(1, 3)
    finish(3, 1)
    finish(3, 3)
    ats.near_y(2)
    finish(2, 1)
    finish(2, 3)
    ats.far_y(1)
    finish(1, 2)
    ats.far_y(3)
    finish(3, 2)
    ats.far_y(2)
    finish(2, 2)
    out_ref[...] = oacc[...].astype(BF16)
    for copy in pending:
        copy.wait_send()


def per_device(
    states, q_weight, kv_weight, o_weight, store_keys, store_values, prefix_len, cache_len, parents
):
    exponent = np.arange(HD, dtype=np.float32) % (HD // 2) * np.float32(-2.0 / HD)
    frequency = np.exp(exponent * np.log(np.float32(ROPE_BASE))).astype(np.float32)
    x = states[0, 0].reshape(2, ROWS // 2, -1)
    any_space = pl.BlockSpec(memory_space=pl.ANY)
    in_vmem = pl.BlockSpec(memory_space=pltpu.VMEM)
    in_smem = pl.BlockSpec(memory_space=pltpu.SMEM)
    dma = pltpu.SemaphoreType.DMA
    out = pl.pallas_call(
        kernel,
        out_shape=jax.ShapeDtypeStruct((ROWS, o_weight.shape[1]), BF16),
        in_specs=[in_smem, in_smem, in_vmem, in_vmem] + [any_space] * 6,
        out_specs=in_vmem,
        scratch_shapes=[
            pltpu.VMEM((16, 2, ROWS // 2, 512), BF16),
            pltpu.VMEM(q_weight.shape, BF16),
            pltpu.VMEM(kv_weight.shape, BF16),
            pltpu.VMEM(o_weight.shape, BF16),
            pltpu.VMEM((4, 4, NODES, 2 * HD), BF16),
            pltpu.VMEM((16, NODES, 2 * HD), BF16),
            pltpu.VMEM((16, ROWS, HD), BF16),
            pltpu.VMEM((16, ROWS, HD), BF16),
            pltpu.VMEM((2, ROWS, HD), BF16),
            pltpu.VMEM((2, 4, NODES, HD), BF16),
            pltpu.VMEM((2, 4, NODES, HD), BF16),
            pltpu.VMEM((ROWS, 2 * HD), F32),
            pltpu.VMEM((2, ROWS, HD), BF16),
            pltpu.VMEM((ROWS, ROWS), BF16),
            pltpu.VMEM((ROWS, HD), F32),
            pltpu.VMEM((ROWS, HD), F32),
            pltpu.VMEM((2, ROWS, HD), F32),
            pltpu.VMEM((2, ROWS, HD), F32),
            pltpu.VMEM((2, ROWS, HD), F32),
            pltpu.VMEM((16, 2, ROWS // 2, 2 * HD), BF16),
            pltpu.VMEM((ROWS, o_weight.shape[1]), F32),
            dma((6,)),
            dma((32,)),
            dma((16, 2)),
            dma((36,)),
            dma((16, 2)),
            dma((2,)),
            dma((16,)),
            dma((16,)),
            dma((4,)),
            dma((4,)),
            dma((2,)),
            dma((32,)),
            dma((16, 2)),
        ],
        compiler_params=pltpu.CompilerParams(
            collective_id=0, has_side_effects=True, vmem_limit_bytes=56 * 2**20
        ),
    )(
        prefix_len, cache_len, parents[0], jnp.asarray(frequency)[None], x, q_weight, kv_weight, o_weight,
        store_keys[0, 0], store_values[0, 0],
    )
    return out[None, None]


def solution(mesh):
    return jax.shard_map(
        per_device,
        mesh=mesh,
        in_specs=(
            P("section", "rep", None, "tp"),
            P(None, "tp"),
            P("tp", None),
            P(None, "tp"),
            P("section", "rep", "tp", None),
            P("section", "rep", "tp", None),
            P(),
            P("rep", None),
            P("rep", None, None),
        ),
        out_specs=P("section", "rep", None, "tp"),
        check_vma=False,
    )
```

time: 365 us -> 108 us (0.30)
  waiting for transfers between devices: 269 us -> 0 us
  Pallas kernels: 0 us -> 106 us
  starting transfers between devices: 33.4 us -> 0 us
  matrix products: 25.7 us -> 0 us
  between operations: 14.2 us -> 0.01 us
  other arithmetic: 14.1 us -> 0 us
  local copies, waits for them, and re-layouts: 8.3 us -> 1.67 us
    all_gather x3 -> x0, waiting for transfers between devices: 169 us -> none  [the longest x1 81.5 us: per_device(): lax.all_gather(inputs, TP, axis=1, tiled=True)]
    pallas_call x0 -> x1, Pallas kernels: none -> 106 us  [per_device(): pl.pallas_call(kernel, out_shape=jax.ShapeDtypeStruct((ROWS, o_weight.sha...]
    all_to_all x7 -> x0, waiting for transfers between devices: 98 us -> none  [the longest x6 79.4 us: exchange_in_order(): lax.all_to_all(tiles, axes[k], split_axis=k, concat_axis=k, tiled=True)]
    all_to_all x7 -> x0, starting transfers between devices: 32.1 us -> none  [the longest x6 25.8 us: exchange_in_order(): lax.all_to_all(tiles, axes[k], split_axis=k, concat_axis=k, tiled=True)]
    dot_general x17 -> x0, matrix products: 25.7 us -> none  [the longest x4 7.26 us: partial_attend(): jnp.dot(weights.astype(jnp.bfloat16).reshape(row_count * group_size, -1),...]
    reduce_sum x4 -> x0, other arithmetic: 4.89 us -> none  [the longest x1 4.27 us: partial_attend(): row_total = jnp.sum(weights, axis=-1)]
  transfers between devices with their start and end apart: 11 -> 0, of which waited for: 10 -> 0; matrix products, arithmetic and copies ran while one was open for 8% -> 0% of each run, Pallas kernels for 0% -> 0%
where the time goes in v1:
time: 108 us
  Pallas kernels  106 us (98%)
  local copies, waits for them, and re-layouts  1.67 us (2%)
    pallas_call x1, Pallas kernels, per_device(): pl.pallas_call(kernel, out_shape=jax.ShapeDtypeStruct((ROWS, o_weight.sha...  106 us

profile of v1, /device:TPU:2, one launch (start us, length us, event | category | flops | bytes accessed | tf_op | source)
XLA Modules:
  0.0 108.1 jit_solution(411212836027638060)
XLA Ops:
  0.0 106.4 %shard_map.100 = bf16[256,512]{1,0:T(8,128)(2,1)} custom-call(s32[8]{0:T(128)} %prefix_ref.1, s32[1,4]{1,0:T(1,128)} %cache_ref.1, s32[4,64]{1,0:T(4,128)} %bitcast.9, f32[1,128]{1,0:T(1,128)} %constant.8.freq_ref, bf16[2,128,512]{2,1,0:T(8,128)(2,1)} %bitcast.6, bf16[8192,256]{1,0:T(8,128)(2,1)} %wq_hbm.1, bf16[512,1024]{1,0:T(8,128)(2,1)} %wkv_hbm.1, ...), custom_call_target="tpu_custom_call" | custom-call | tf_op jit(solution)/shard_map/pallas_call | solution.py:448
  106.5 1.7 %copy.12 = bf16[1,1,256,512]{3,2,1,0:T(8,128)(2,1)} copy(bf16[1,1,256,512]{3,2,1,0:T(8,128)(2,1)} %bitcast.5) | data formatting | bytes 524288

commit v2 on v1

--- a/solution.py
+++ b/solution.py
@@ -22,35 +22,49 @@
     return dy * 4 + dz
 
 
-class Exchange:
-    def __init__(self, view, send_sems, recv_sems, at, pending):
-        self.view, self.send_sems, self.recv_sems = view, send_sems, recv_sems
-        self.at, self.pending, self.used = at, pending, 0
-
-    def send(self, src, dst_slot, half, dz, dy):
+class Links:
+    def __init__(self, send_sems):
+        self.send_sems, self.started = send_sems, []
+
+    def send(self, src, dst, recv_sem, device):
         copy = pltpu.make_async_remote_copy(
             src_ref=src,
-            dst_ref=self.view(dst_slot, half),
-            send_sem=self.send_sems.at[self.used],
-            recv_sem=self.recv_sems.at[dst_slot, half],
-            device_id={"tp": self.at(dz, dy)},
+            dst_ref=dst,
+            send_sem=self.send_sems.at[len(self.started)],
+            recv_sem=recv_sem,
+            device_id=device,
             device_id_type=MESH,
         )
-        self.used += 1
         copy.start()
-        self.pending.append(copy)
-
-    def arrived(self, dz, dy, half):
-        slot = slot_of(dz, dy)
-        view = self.view(slot, half)
+        self.started.append(copy)
+
+    def arrived(self, view, recv_sem, device):
         pltpu.make_async_remote_copy(
             src_ref=view,
             dst_ref=view,
             send_sem=self.send_sems.at[0],
-            recv_sem=self.recv_sems.at[slot, half],
-            device_id={"tp": self.at(1, 0)},
+            recv_sem=recv_sem,
+            device_id=device,
             device_id_type=MESH,
         ).wait_recv()
+
+    def finish(self):
+        for copy in self.started:
+            copy.wait_send()
+
+
+class Exchange:
+    def __init__(self, links, view, recv_sems, at):
+        self.links, self.view, self.recv_sems, self.at = links, view, recv_sems, at
+
+    def send(self, src, dst_slot, half, dz, dy):
+        self.links.send(
+            src, self.view(dst_slot, half), self.recv_sems.at[dst_slot, half], {"tp": self.at(dz, dy)}
+        )
+
+    def arrived(self, dz, dy, half):
+        slot = slot_of(dz, dy)
+        self.links.arrived(self.view(slot, half), self.recv_sems.at[slot, half], {"tp": self.at(1, 0)})
 
     def own_z(self, half):
         self.send(self.view(0, half), slot_of(1, 0), half, 1, 0)
@@ -93,17 +107,23 @@
 def kernel(
     prefix_ref, cache_ref, parents_ref, freq_ref, x_hbm, wq_hbm, wkv_hbm, wo_hbm, sk_hbm, sv_hbm,
     out_ref,
-    xg, wq, wkv, wo, kvps, kvpr, kg, vg, relay, nkv, tail, qacc, qh, closed, cos_ref, sin_ref,
-    top_ref, total_ref, mix_ref, ag, oacc,
-    local, x_send, x_recv, k_send, k_recv, r_recv, p_send, p_recv, n_send, n_recv, t_sem, a_send, a_recv,
+    xg, wl, wg, wkv, wo, kvps, kvpr, kvqs, kvqr, kg, vg, relay, nkv, tail, qacc, qs, qr, qh,
+    closed, cos_ref, sin_ref, top_ref, total_ref, mix_ref, ag, oacc,
+    local, send_sems, x_recv, k_recv, r_recv, p_recv, u_recv, n_recv, t_recv, a_recv,
+    f_recv, g_recv, w_recv, q_recv,
 ):
     tp = lax.axis_index("tp")
     sec = lax.axis_index("section")
     rep = lax.axis_index("rep")
     z, y = tp // 4, tp % 4
+    lane_x = rep % 4
+    twin = {"section": 1 - sec}
 
     def at(dz, dy):
         return ((z + dz + 4) % 4) * 4 + (y + dy + 4) % 4
+
+    def beside(dx):
+        return {"rep": rep - lane_x + (lane_x + dx + 4) % 4}
 
     def head_cols(dz):
         return pl.ds(pl.multiple_of(((z + dz + 4) % 4) * HD, HD), HD)
@@ -113,30 +133,22 @@
         copy.start()
         return copy
 
+    barrier = pltpu.get_barrier_semaphore()
+    for dz, dy in ((1, 0), (2, 0), (3, 0), (0, 1), (0, 2), (0, 3)):
+        pl.semaphore_signal(barrier, inc=1, device_id={"tp": at(dz, dy)}, device_id_type=MESH)
+    for device in (beside(1), beside(-1), twin):
+        pl.semaphore_signal(barrier, inc=1, device_id=device, device_id_type=MESH)
+
     x_in = load(x_hbm, xg.at[0], 0)
     wkv_in = load(wkv_hbm, wkv, 1)
-    wq_in = load(wq_hbm, wq, 2)
-    k_in = load(sk_hbm.at[:, head_cols(0)], kg.at[0], 3)
-    v_in = load(sv_hbm.at[:, head_cols(0)], vg.at[0], 4)
-    wo_in = load(wo_hbm, wo, 5)
-
-    barrier = pltpu.get_barrier_semaphore()
-    peers = [(dz, dy) for dy in range(4) for dz in range(4) if (dz, dy) != (0, 0)]
-    for dz, dy in peers:
-        pl.semaphore_signal(barrier, inc=1, device_id={"tp": at(dz, dy)}, device_id_type=MESH)
-    pl.semaphore_signal(barrier, inc=1, device_id={"section": 1 - sec}, device_id_type=MESH)
-    pl.semaphore_wait(barrier, 16)
-
-    pending = []
-    xs = Exchange(lambda s, h: xg.at[s, h], x_send, x_recv, at, pending)
-    ks = Exchange(lambda s, h: (kg if h == 0 else vg).at[s], k_send, k_recv, at, pending)
-    ats = Exchange(lambda s, h: ag.at[s, h], a_send, a_recv, at, pending)
+    k_in = load(sk_hbm.at[:, head_cols(0)], kg.at[0], 2)
+    v_in = load(sv_hbm.at[:, head_cols(0)], vg.at[0], 3)
+    wl_in = [
+        load(wq_hbm.at[pl.ds(pl.multiple_of((n * 4 + y) * 512, 512), 512)], wl.at[n], 4 + n) for n in range(4)
+    ]
+    wo_in = load(wo_hbm, wo, 8)
 
     x_in.wait()
-    for half in range(2):
-        xs.own_z(half)
-        xs.along_y(0, half)
-
     wkv_in.wait()
     own_x = xg[0].reshape(ROWS, -1)
     for head in range(4):
@@ -144,40 +156,6 @@
             cols = pl.ds(kind * 512 + head * HD, HD)
             part = dot(own_x, wkv[:, cols]).astype(BF16)
             kvps[:, head, :, pl.ds(kind * HD, HD)] = part.reshape(4, NODES, HD)
-
-    for dz in (1, -1):
-        ks.send(sk_hbm.at[:, head_cols(dz)], slot_of(dz % 4, 0), 0, dz, 0)
-        ks.send(sv_hbm.at[:, head_cols(dz)], slot_of(dz % 4, 0), 1, dz, 0)
-
-    def to_relay(src, half, dz):
-        copy = pltpu.make_async_remote_copy(
-            src_ref=src,
-            dst_ref=relay.at[half],
-            send_sem=k_send.at[ks.used],
-            recv_sem=r_recv.at[half],
-            device_id={"tp": at(dz, 0)},
-            device_id_type=MESH,
-        )
-        ks.used += 1
-        copy.start()
-        pending.append(copy)
-        return copy
-
-    relays = [to_relay(sk_hbm.at[:, head_cols(2)], 0, 1), to_relay(sv_hbm.at[:, head_cols(2)], 1, -1)]
-
-    parts_in = []
-    for n, (dz, dy) in enumerate(peers):
-        copy = pltpu.make_async_remote_copy(
-            src_ref=kvps.at[(y + dy) % 4, (z + dz) % 4],
-            dst_ref=kvpr.at[slot_of(dz, dy)],
-            send_sem=p_send.at[n],
-            recv_sem=p_recv.at[slot_of(dz, dy)],
-            device_id={"tp": at(dz, dy)},
-            device_id_type=MESH,
-        )
-        copy.start()
-        pending.append(copy)
-        parts_in.append(copy)
 
     row = iota((ROWS, ROWS), 0)
     col = iota((ROWS, ROWS), 1)
@@ -212,111 +190,146 @@
     def rotate(v, cosine, sine):
         return v * cosine + pltpu.roll(v, HD // 2, 1) * sine
 
-    wq_in.wait()
-
-    def project(dz, dy, first=False):
-        source = pl.multiple_of(at(-dz, -dy) * 512, 512)
-        part = dot(xg[slot_of(dz, dy)].reshape(ROWS, -1), wq[pl.ds(source, 512), :])
-        qacc[...] = part if first else qacc[...] + part
-
-    xs.near_y(0)
-    project(0, 0, True)
+    k_in.wait()
+    v_in.wait()
+    for copy in wl_in:
+        copy.wait()
+    wo_in.wait()
+    pl.semaphore_wait(barrier, 9)
+
+    links = Links(send_sems)
+    xs = Exchange(links, lambda s, h: xg.at[s, h], x_recv, at)
+    ks = Exchange(links, lambda s, h: (kg if h == 0 else vg).at[s], k_recv, at)
+    ats = Exchange(links, lambda s, h: ag.at[s, h], a_recv, at)
+
+    for dy in (1, 3, 2):
+        start = (lane_x * 4 + (y + dy) % 4) * 512 + sec * 256
+        for half in range(2):
+            source = wq_hbm.at[pl.ds(pl.multiple_of(start + half * 128, 128), 128)]
+            links.send(source, wg.at[dy - 1, lane_x, sec, half], f_recv.at[dy - 1, half], {"tp": at(0, dy)})
+    for half in range(2):
+        xs.own_z(half)
+    for dy in (1, 3, 2):
+        links.send(kvps.at[(y + dy) % 4], kvpr.at[dy - 1], p_recv.at[dy - 1], {"tp": at(0, dy)})
+    for half in range(2):
+        ks.along_y(0, half)
+
+    def weight(dy, dx, half):
+        return wg.at[dy - 1, (lane_x - dx + 4) % 4, sec, half]
+
+    def to_twin(dy, dx):
+        part = wg.at[dy - 1, (lane_x - dx + 4) % 4, sec]
+        links.send(part, part, w_recv.at[dy - 1, dx], twin)
+
+    def weight_in(dy, dx, half):
+        links.arrived(weight(dy, dx, half), g_recv.at[dy - 1, dx, half], twin)
+
+    def fetched(dy):
+        for half in range(2):
+            part = weight(dy, 0, half)
+            links.arrived(part, f_recv.at[dy - 1, half], twin)
+            links.send(part, part, g_recv.at[dy - 1, 1, half], beside(1))
+            links.send(part, part, g_recv.at[dy - 1, 3, half], beside(-1))
+        to_twin(dy, 0)
+
+    def near_x(dy):
+        weight_in(dy, 1, 0)
+        links.send(weight(dy, 1, 0), weight(dy, 1, 0), g_recv.at[dy - 1, 2, 0], beside(1))
+        weight_in(dy, 3, 0)
+        weight_in(dy, 3, 1)
+        links.send(weight(dy, 3, 1), weight(dy, 3, 1), g_recv.at[dy - 1, 2, 1], beside(-1))
+        to_twin(dy, 3)
+        weight_in(dy, 1, 1)
+        to_twin(dy, 1)
+
+    def far_x(dy):
+        weight_in(dy, 2, 0)
+        weight_in(dy, 2, 1)
+        to_twin(dy, 2)
+
+    def from_twin(dy):
+        for dx in range(4):
+            part = wg.at[dy - 1, (lane_x - dx + 4) % 4, 1 - sec]
+            links.arrived(part, w_recv.at[dy - 1, dx], twin)
+
+    fetched(1)
+    fetched(3)
     xs.arrived(1, 0, 0)
     xs.relay_z(0)
-    xs.along_y(1, 0)
     xs.arrived(3, 0, 0)
-    xs.along_y(3, 0)
+    fetched(2)
+    near_x(1)
     xs.arrived(3, 0, 1)
     xs.relay_z(1)
-    xs.along_y(3, 1)
     xs.arrived(1, 0, 1)
-    xs.along_y(1, 1)
-    project(0, 1)
-    project(0, 3)
-    project(1, 0)
-    project(3, 0)
-    xs.far_y(0)
-    project(0, 2)
-    for half in range(2):
-        relays[half].wait_recv()
+
+    links.send(sk_hbm.at[:, head_cols(2)], relay.at[0], r_recv.at[0], {"tp": at(1, 0)})
+    links.send(sv_hbm.at[:, head_cols(2)], relay.at[1], r_recv.at[1], {"tp": at(-1, 0)})
+    for dz in (1, -1):
+        ks.send(sk_hbm.at[:, head_cols(dz)], slot_of(dz % 4, 0), 0, dz, 0)
+        ks.send(sv_hbm.at[:, head_cols(dz)], slot_of(dz % 4, 0), 1, dz, 0)
+
+    near_x(3)
+
+    for dy in range(1, 4):
+        links.arrived(kvpr.at[dy - 1], p_recv.at[dy - 1], twin)
+    for n in range(4):
+        fresh = kvps[y, n].astype(F32)
+        for dy in range(1, 4):
+            fresh = fresh + kvpr[dy - 1, n].astype(F32)
+        kvqs[n] = fresh
+    near_x(2)
+    far_x(1)
+    far_x(3)
+    for dz in range(1, 4):
+        links.send(kvqs.at[(z + dz) % 4], kvqr.at[dz - 1], u_recv.at[dz - 1], {"tp": at(dz, 0)})
+    ks.near_y(0)
+    for half in range(2):
+        xs.arrived(2, 0, half)
+
+    def project(dy):
+        total = 0.0
+        for dz in range(4):
+            from_z = (z - dz + 4) % 4
+            weights = wl[from_z] if dy == 0 else wg[dy - 1, from_z].reshape(512, 2 * HD)
+            total = total + dot(xg[dz].reshape(ROWS, -1), weights)
+        return total
+
+    for dy in (1, 3):
+        from_twin(dy)
+        qs[dy - 1] = project(dy)
+        links.send(qs.at[dy - 1], qr.at[dy - 1], q_recv.at[dy - 1], {"tp": at(0, -dy)})
+    for half in range(2):
+        links.arrived(relay.at[half], r_recv.at[half], twin)
         ks.send(relay.at[half], slot_of(2, 0), half, 1 if half == 0 else -1, 0)
-    xs.near_y(1)
-    xs.near_y(3)
-    for half in range(2):
-        xs.arrived(2, 0, half)
-        xs.along_y(2, half)
-    project(1, 1)
-    project(1, 3)
-    project(3, 1)
-    project(3, 3)
-    project(2, 0)
-
-    k_in.wait()
-    v_in.wait()
-    for dz in (0, 1, 3):
+    far_x(2)
+    from_twin(2)
+    qs[1] = project(2)
+    links.send(qs.at[1], qr.at[1], q_recv.at[1], {"tp": at(0, -2)})
+    qacc[...] = project(0)
+
+    for dz in (1, 3):
         for half in range(2):
-            if dz:
-                ks.arrived(dz, 0, half)
+            ks.arrived(dz, 0, half)
             ks.along_y(dz, half)
-
-    for copy in parts_in:
-        copy.wait_recv()
-    fresh = kvps[y, z].astype(F32)
-    for dz, dy in peers:
-        fresh = fresh + kvpr[slot_of(dz, dy)].astype(F32)
+    for dz in range(1, 4):
+        links.arrived(kvqr.at[dz - 1], u_recv.at[dz - 1], twin)
+    fresh = kvqs[z] + kvqr[0] + kvqr[1] + kvqr[2]
     rows = pl.ds(pl.multiple_of(y * NODES, NODES), NODES)
     fresh_keys = rotate(fresh[:, :HD], cos_ref[rows, :], sin_ref[rows, :])
     nkv[0, y] = fresh_keys.astype(BF16)
     nkv[1, y] = fresh[:, HD:].astype(BF16)
-
-    xs.far_y(1)
-    xs.far_y(3)
-    project(1, 2)
-    project(3, 2)
-
-    news = []
-    for dy in range(1, 4):
-        copy = pltpu.make_async_remote_copy(
-            src_ref=nkv.at[:, y],
-            dst_ref=nkv.at[:, y],
-            send_sem=n_send.at[dy],
-            recv_sem=n_recv.at[dy],
-            device_id={"tp": at(0, dy)},
-            device_id_type=MESH,
-        )
-        copy.start()
-        pending.append(copy)
-
-    xs.near_y(2)
-    project(2, 1)
-    project(2, 3)
     for half in range(2):
         ks.arrived(2, 0, half)
         ks.along_y(2, half)
     for dy in range(1, 4):
-        piece = nkv.at[:, (y + 4 - dy) % 4]
-        pltpu.make_async_remote_copy(
-            src_ref=piece,
-            dst_ref=piece,
-            send_sem=n_send.at[dy],
-            recv_sem=n_recv.at[dy],
-            device_id={"tp": at(0, dy)},
-            device_id_type=MESH,
-        ).wait_recv()
-    swap = pltpu.make_async_remote_copy(
-        src_ref=nkv,
-        dst_ref=tail,
-        send_sem=t_sem.at[0],
-        recv_sem=t_sem.at[1],
-        device_id={"section": 1 - sec},
-        device_id_type=MESH,
-    )
-    swap.start()
-    pending.append(swap)
-    xs.far_y(2)
-    project(2, 2)
+        links.send(nkv.at[:, y], nkv.at[:, y], n_recv.at[dy], {"tp": at(0, dy)})
+    for dy in range(1, 4):
+        links.arrived(qr.at[dy - 1], q_recv.at[dy - 1], twin)
     for head in range(2):
-        qh[head] = rotate(qacc[:, head * HD : (head + 1) * HD], cos_ref[...], sin_ref[...]).astype(BF16)
+        cols = pl.ds(head * HD, HD)
+        query = qacc[:, cols] + qr[0, :, cols] + qr[1, :, cols] + qr[2, :, cols]
+        qh[head] = rotate(query, cos_ref[...], sin_ref[...]).astype(BF16)
 
     seq_wide = row // NODES
 
@@ -368,17 +381,24 @@
 
         return (lambda: kg[slot], lambda: vg[slot], visible)
 
+    ks.near_y(1)
+    ks.near_y(3)
+    for dy in range(1, 4):
+        links.arrived(nkv.at[:, (y + 4 - dy) % 4], n_recv.at[dy], twin)
+    links.send(nkv, tail, t_recv.at[0], twin)
     attend([(lambda: nkv[0].reshape(ROWS, HD), lambda: nkv[1].reshape(ROWS, HD), new_visible)], True)
-    for dz in (0, 1, 3, 2):
-        ks.near_y(dz)
+    ks.near_y(2)
     attend([stored(dz, 0) for dz in range(4)])
-    swap.wait_recv()
+    ks.far_y(0)
+    attend([stored(0, 1), stored(0, 3), stored(0, 2)])
+    attend([stored(1, 1), stored(1, 3), stored(3, 1), stored(3, 3)])
+    links.arrived(tail, t_recv.at[0], twin)
     attend([(lambda: tail[0].reshape(ROWS, HD), lambda: tail[1].reshape(ROWS, HD), tail_visible)])
-    attend([stored(dz, 1) for dz in range(4)])
-    attend([stored(dz, 3) for dz in range(4)])
-    for dz in range(4):
-        ks.far_y(dz)
-    attend([stored(dz, 2) for dz in range(4)])
+    ks.far_y(1)
+    ks.far_y(3)
+    attend([stored(2, 1), stored(2, 3), stored(1, 2), stored(3, 2)])
+    ks.far_y(2)
+    attend([stored(2, 2)])
     for head in range(2):
         done = (mix_ref[head] / total_ref[head]).astype(BF16)
         ag[0, :, :, head * HD : (head + 1) * HD] = done.reshape(2, ROWS // 2, HD)
@@ -386,7 +406,6 @@
     for half in range(2):
         ats.own_z(half)
         ats.along_y(0, half)
-    wo_in.wait()
 
     def finish(dz, dy, first=False):
         source = pl.multiple_of(at(-dz, -dy) * 256, 256)
@@ -431,8 +450,7 @@
     ats.far_y(2)
     finish(2, 2)
     out_ref[...] = oacc[...].astype(BF16)
-    for copy in pending:
-        copy.wait_send()
+    links.finish()
 
 
 def per_device(
@@ -451,18 +469,23 @@
         in_specs=[in_smem, in_smem, in_vmem, in_vmem] + [any_space] * 6,
         out_specs=in_vmem,
         scratch_shapes=[
-            pltpu.VMEM((16, 2, ROWS // 2, 512), BF16),
-            pltpu.VMEM(q_weight.shape, BF16),
+            pltpu.VMEM((4, 2, ROWS // 2, 512), BF16),
+            pltpu.VMEM((4, 512, 2 * HD), BF16),
+            pltpu.VMEM((3, 4, 2, 2, 128, 2 * HD), BF16),
             pltpu.VMEM(kv_weight.shape, BF16),
             pltpu.VMEM(o_weight.shape, BF16),
             pltpu.VMEM((4, 4, NODES, 2 * HD), BF16),
-            pltpu.VMEM((16, NODES, 2 * HD), BF16),
+            pltpu.VMEM((3, 4, NODES, 2 * HD), BF16),
+            pltpu.VMEM((4, NODES, 2 * HD), F32),
+            pltpu.VMEM((3, NODES, 2 * HD), F32),
             pltpu.VMEM((16, ROWS, HD), BF16),
             pltpu.VMEM((16, ROWS, HD), BF16),
             pltpu.VMEM((2, ROWS, HD), BF16),
             pltpu.VMEM((2, 4, NODES, HD), BF16),
             pltpu.VMEM((2, 4, NODES, HD), BF16),
             pltpu.VMEM((ROWS, 2 * HD), F32),
+            pltpu.VMEM((3, ROWS, 2 * HD), F32),
+            pltpu.VMEM((3, ROWS, 2 * HD), F32),
             pltpu.VMEM((2, ROWS, HD), BF16),
             pltpu.VMEM((ROWS, ROWS), BF16),
             pltpu.VMEM((ROWS, HD), F32),
@@ -472,19 +495,20 @@
             pltpu.VMEM((2, ROWS, HD), F32),
             pltpu.VMEM((16, 2, ROWS // 2, 2 * HD), BF16),
             pltpu.VMEM((ROWS, o_weight.shape[1]), F32),
-            dma((6,)),
-            dma((32,)),
-            dma((16, 2)),
-            dma((36,)),
+            dma((9,)),
+            dma((144,)),
+            dma((4, 2)),
             dma((16, 2)),
             dma((2,)),
-            dma((16,)),
-            dma((16,)),
+            dma((3,)),
+            dma((3,)),
             dma((4,)),
-            dma((4,)),
-            dma((2,)),
-            dma((32,)),
+            dma((1,)),
             dma((16, 2)),
+            dma((3, 2)),
+            dma((3, 4, 2)),
+            dma((3, 4)),
+            dma((3,)),
         ],
         compiler_params=pltpu.CompilerParams(
             collective_id=0, has_side_effects=True, vmem_limit_bytes=56 * 2**20

time: 108 us -> 94.8 us (0.88)
  the two profiles are of different devices: /device:TPU:2 before, /device:TPU:32 now
where the time goes in v2:
time: 94.8 us; the launch traced here: 94.6 us
  Pallas kernels  93 us (98%)
  local copies, waits for them, and re-layouts  1.67 us (2%)
    pallas_call x1, Pallas kernels, per_device(): pl.pallas_call(kernel, out_shape=jax.ShapeDtypeStruct((ROWS, o_weight.sha...  93 us

profile of v2, /device:TPU:32, one launch (start us, length us, event | category | flops | bytes accessed | tf_op | source)
XLA Modules:
  0.0 94.6 jit_solution(4771511843727462707)
XLA Ops:
  0.0 93.0 %shard_map.100 = bf16[256,512]{1,0:T(8,128)(2,1)} custom-call(s32[8]{0:T(128)} %prefix_ref.1, s32[1,4]{1,0:T(1,128)} %cache_ref.1, s32[4,64]{1,0:T(4,128)} %bitcast.9, f32[1,128]{1,0:T(1,128)} %constant.8.freq_ref, bf16[2,128,512]{2,1,0:T(8,128)(2,1)} %bitcast.6, bf16[8192,256]{1,0:T(8,128)(2,1)} %wq_hbm.1, bf16[512,1024]{1,0:T(8,128)(2,1)} %wkv_hbm.1, ...), custom_call_target="tpu_custom_call" | custom-call | tf_op jit(solution)/shard_map/pallas_call | solution.py:466
  93.0 1.7 %copy.12 = bf16[1,1,256,512]{3,2,1,0:T(8,128)(2,1)} copy(bf16[1,1,256,512]{3,2,1,0:T(8,128)(2,1)} %bitcast.5) | data formatting | bytes 524288
